TPU v7x, 256 devices: a whole 4x4x8 slice. The times are simulated.
256 devices in a mesh: shard: 64 (over z, x, core), model: 4 (over y).
Axes of the slice: x: 4, y: 4, z: 8, core: 2. Of those that a mesh axis runs over, the one named last changes fastest.
Arguments:
- grad_stack: float32 [512, 128, 2048], P(None, 'shard', 'model'), may hold values from -6 to 6
- moment_stack: float32 [512, 128, 2048], P(None, 'shard', 'model'), may hold values from -6 to 6
- weight_stack: float32 [512, 128, 2048], P(None, 'shard', 'model'), may hold values from -0.1875 to 0.1875
Outputs:
- new_weights: float32 [512, 128, 2048], P(None, 'shard', 'model')
- new_momentum: float32 [512, 128, 2048], P(None, 'shard', 'model')
All inputs are finite; a program needn't handle non-finite values.
Results may differ from a plain program's by a relative error of at most 0.00021.
Values sent between devices are 32-bit elements; how exact they have to be, the bound alone decides.
A program may use at most 64 MiB of HBM per device.

v0:
```python
import jax
import jax.numpy as jnp
from jax import lax
from jax.sharding import PartitionSpec as P

ITERS = 5
hold_rate = 0.95
learn_rate = 1.0
decay_rate = 0.1


def on_device(grad_stack, moment_stack, weight_stack):
    new_momentum = hold_rate * moment_stack + grad_stack
    moved = lax.all_to_all(new_momentum, "shard", split_axis=0, concat_axis=1, tiled=True)
    whole = lax.all_to_all(moved, "model", split_axis=0, concat_axis=2, tiled=True)
    iterate = whole * lax.rsqrt(jnp.sum(whole * whole, axis=(1, 2), keepdims=True) + 1e-06)
    for step in range(ITERS):
        gram = jnp.einsum("mik,mjk->mij", iterate, iterate, precision=lax.Precision.HIGHEST)
        mixed = -4.775 * gram + 2.0315 * jnp.einsum(
            "mij,mjk->mik", gram, gram, precision=lax.Precision.HIGHEST
        )
        iterate = 3.4445 * iterate + jnp.einsum(
            "mij,mjk->mik", mixed, iterate, precision=lax.Precision.HIGHEST
        )
    iterate = lax.all_to_all(iterate, "model", split_axis=2, concat_axis=0, tiled=True)
    back = lax.all_to_all(iterate, "shard", split_axis=1, concat_axis=0, tiled=True)
    new_weights = (1.0 - learn_rate * decay_rate) * weight_stack - learn_rate * back
    return (new_weights, new_momentum)


def solution(mesh):
    in_specs = (P(None, "shard", "model"), P(None, "shard", "model"), P(None, "shard", "model"))
    out_specs = (P(None, "shard", "model"), P(None, "shard", "model"))
    return jax.shard_map(
        on_device, mesh=mesh, in_specs=in_specs, out_specs=out_specs, check_vma=False
    )
```

profile of v0, /device:TPU:2, one launch (start us, length us, event | category | flops | bytes accessed | tf_op | source)
XLA Modules:
  0.0 220.1 jit_solution(1098745697749330971)
XLA Ops:
  0.6 3.7 %multiply_add_fusion = f32[512,2,512]{2,1,0:T(2,128)S(1)} fusion(f32[512,2,512]{2,1,0:T(2,128)} %param.3, f32[512,2,512]{2,1,0:T(2,128)} %param.4), kind=kLoop, calls=%fused_computation.9 | loop fusion | flops 1048576 | bytes 6291456 | tf_op jit(solution)/shard_map/add | solution.py:13
  4.3 0.0 copy-start
  4.3 63.1 %all_to_all.72 = f32[512,2,512]{2,1,0:T(2,128)S(1)} all-to-all(f32[512,2,512]{2,1,0:T(2,128)S(1)} %multiply_add_fusion), channel_id=1, replica_groups=mesh['shard'=64,'model'=4] {'shard'}, dimensions={0} | all-to-all | bytes 4194304 | tf_op jit(solution)/shard_map/all_to_all | solution.py:14
  67.4 0.4 copy.46
  67.8 0.2 copy.31
  68.0 1.2 copy.32
  69.2 29.1 %all_to_all.73 = f32[8,128,512]{2,1,0:T(8,128)S(1)} all-to-all(f32[8,128,512]{2,1,0:T(8,128)S(1)} %copy.32), channel_id=1, replica_groups=mesh['shard'=64,'model'=4] {'model'}, dimensions={0} | all-to-all | bytes 4194304 | tf_op jit(solution)/shard_map/all_to_all | solution.py:15
  98.3 0.4 multiply_reduce_fusion
  98.7 0.2 copy.40
  98.9 2.3 %fusion = f32[2,128,128]{2,1,0:T(8,128)S(1)} fusion(f32[2,128,2048]{2,1,0:T(8,128)S(1)} %bitcast.47, f32[2]{0:T(128)S(1)} %add_rsqrt_fusion), kind=kOutput, calls=%fused_computation.10 | convolution fusion | flops 805830656 | bytes 2228232 | tf_op jit(solution)/shard_map/mik,mjk->mij/dot_general | solution.py:18
  101.2 0.3 fusion.7
  101.5 2.1 convolution_add_fusion.4
  103.6 2.0 fusion.10
  105.7 0.3 fusion.6
  105.9 2.1 convolution_add_fusion.3
  108.1 2.0 fusion.11
  110.1 0.3 fusion.5
  110.4 2.3 %convolution_add_fusion.2 = f32[2,128,2048]{2,1,0:T(8,128)S(1)} fusion(f32[2,128,128]{2,1,0:T(8,128)S(1)} %fusion.5, f32[2,128,2048]{2,1,0:T(8,128)S(1)} %convolution_add_fusion.3), kind=kOutput, calls=%fused_computation.2 | convolution fusion | flops 806354944 | bytes 4325376 | tf_op jit(solution)/shard_map/mij,mjk->mik/dot_general | solution.py:22
  112.7 2.0 fusion.12
  114.8 0.3 fusion.4
  115.0 2.1 convolution_add_fusion.1
  117.1 2.0 fusion.13
  119.2 0.3 fusion.3
  119.4 2.1 convolution_add_fusion
  121.5 2.3 %copy.34 = f32[2,128,2048]{1,0,2:T(2,128)} copy(f32[2,128,2048]{2,1,0:T(8,128)S(1)} %convolution_add_fusion) | data formatting | bytes 4194304 | tf_op jit(solution)/shard_map/add | solution.py:22
  123.9 27.5 %all_to_all.74 = f32[2,128,2048]{1,0,2:T(2,128)S(1)} all-to-all(f32[2,128,2048]{1,0,2:T(2,128)} %copy.34), channel_id=1, replica_groups=mesh['shard'=64,'model'=4] {'model'}, dimensions={2} | all-to-all | bytes 4194304 | tf_op jit(solution)/shard_map/all_to_all | solution.py:25
  151.4 0.1 copy.35
  151.5 1.8 copy.36
  153.3 2.8 %copy.37 = f32[8,128,512]{2,0,1:T(8,128)S(1)} copy(f32[8,128,512]{2,1,0:T(8,128)} %bitcast.55) | data formatting | bytes 4194304 | tf_op jit(solution)/shard_map/all_to_all | solution.py:25
  156.2 60.4 %all_to_all.75 = f32[8,128,512]{2,0,1:T(8,128)S(1)} all-to-all(f32[8,128,512]{2,0,1:T(8,128)S(1)} %copy.37), channel_id=1, replica_groups=mesh['shard'=64,'model'=4] {'shard'}, dimensions={1} | all-to-all | bytes 4194304 | tf_op jit(solution)/shard_map/all_to_all | solution.py:26
  216.6 0.6 bitcast_subtract_fusion
  217.2 2.9 %copy.39 = f32[512,2,512]{2,1,0:T(2,128)} copy(f32[512,2,512]{2,0,1:T(8,128)S(1)} %bitcast_subtract_fusion) | data formatting | bytes 4194304
  (4 shorter events, 0.0 us)
Async XLA Ops:
  4.3 63.5 %copy-start = (f32[512,2,512]{2,1,0:T(2,128)}, f32[512,2,512]{2,1,0:T(2,128)S(1)}, u32[]{:S(2)}) copy-start(f32[512,2,512]{2,1,0:T(2,128)S(1)} %multiply_add_fusion) | copy-start | bytes 6291460
  156.1 60.5 %copy-start.1 = (f32[512,2,512]{2,1,0:T(2,128)S(1)}, f32[512,2,512]{2,1,0:T(2,128)}, u32[]{:S(2)}) copy-start(f32[512,2,512]{2,1,0:T(2,128)} %param.5) | copy-start | bytes 6291460
where the time goes:
time: 220 us
  blocking collectives  180 us (82%)
  matrix products  22.5 us (10%)
  local copies, waits for them, and re-layouts  12.1 us (6%)
  other arithmetic  4.62 us (2%)
    all_to_all x1, blocking collectives, on_device(): lax.all_to_all(new_momentum, 'shard', split_axis=0, concat_axis=1, tiled=...  63.1 us
    all_to_all x1, blocking collectives, on_device(): lax.all_to_all(iterate, 'shard', split_axis=1, concat_axis=0, tiled=True)  60.4 us
    all_to_all x1, blocking collectives, on_device(): lax.all_to_all(moved, 'model', split_axis=0, concat_axis=2, tiled=True)  29.1 us
    all_to_all x1, blocking collectives, on_device(): lax.all_to_all(iterate, 'model', split_axis=2, concat_axis=0, tiled=True)  27.5 us
    dot_general x5, matrix products, on_device(): jnp.einsum('mij,mjk->mik', mixed, iterate, precision=lax.Precision.HIGHEST)  10.7 us
    dot_general x5, matrix products, on_device(): jnp.einsum('mik,mjk->mij', iterate, iterate, precision=lax.Precision.HIGH...  10.4 us
    all_to_all x3, local copies, waits for them, and re-layouts, on_device(): lax.all_to_all(iterate, 'model', split_axis=2, concat_axis=0, tiled=True)  4.76 us

commit v1 on v0

--- a/solution.py
+++ b/solution.py
@@ -7,6 +7,13 @@
 hold_rate = 0.95
 learn_rate = 1.0
 decay_rate = 0.1
+
+
+def exchange_blocks(value, name, split, join):
+    devices = lax.axis_size(name)
+    pieces = jnp.stack(jnp.split(value, devices, axis=split), axis=0)
+    pieces = lax.all_to_all(pieces, name, split_axis=0, concat_axis=0)
+    return jnp.concatenate(pieces, axis=join)
 
 
 def on_device(grad_stack, moment_stack, weight_stack):
@@ -23,7 +30,7 @@
             "mij,mjk->mik", mixed, iterate, precision=lax.Precision.HIGHEST
         )
     iterate = lax.all_to_all(iterate, "model", split_axis=2, concat_axis=0, tiled=True)
-    back = lax.all_to_all(iterate, "shard", split_axis=1, concat_axis=0, tiled=True)
+    back = exchange_blocks(iterate, "shard", 1, 0)
     new_weights = (1.0 - learn_rate * decay_rate) * weight_stack - learn_rate * back
     return (new_weights, new_momentum)
 

time: 220 us -> 249 us (1.13)
  local copies, waits for them, and re-layouts: 12.1 us -> 36.9 us
  other arithmetic: 4.62 us -> 7.29 us
    unnamed x5 -> x69, local copies, waits for them, and re-layouts: 2.95 us -> 30.5 us
    all_to_all x3 -> x2, local copies, waits for them, and re-layouts: 4.76 us -> 1.95 us  [on_device(): lax.all_to_all(iterate, 'model', split_axis=2, concat_axis=0, tiled=True)]
    sub x1, other arithmetic: 0.59 us -> 3.25 us  [on_device(): (1.0 - learn_rate * decay_rate) * weight_stack - learn_rate * back]
where the time goes in v1:
time: 249 us; the launch traced here: 248 us
  blocking collectives  180 us (72%)
  local copies, waits for them, and re-layouts  36.9 us (15%)
  matrix products  22.5 us (9%)
  other arithmetic  7.29 us (3%)
    all_to_all x1, blocking collectives, on_device(): lax.all_to_all(new_momentum, 'shard', split_axis=0, concat_axis=1, tiled=...  63.1 us
    all_to_all x1, blocking collectives, exchange_blocks(): pieces = lax.all_to_all(pieces, name, split_axis=0, concat_axis=0)  60.4 us
    unnamed x69, local copies, waits for them, and re-layouts  30.5 us
    all_to_all x1, blocking collectives, on_device(): lax.all_to_all(moved, 'model', split_axis=0, concat_axis=2, tiled=True)  29.1 us
    all_to_all x1, blocking collectives, on_device(): lax.all_to_all(iterate, 'model', split_axis=2, concat_axis=0, tiled=True)  27.5 us
    dot_general x5, matrix products, on_device(): jnp.einsum('mij,mjk->mik', mixed, iterate, precision=lax.Precision.HIGHEST)  10.7 us
    dot_general x5, matrix products, on_device(): jnp.einsum('mik,mjk->mij', iterate, iterate, precision=lax.Precision.HIGH...  10.4 us

profile of v1, /device:TPU:2, one launch (start us, length us, event | category | flops | bytes accessed | tf_op | source)
XLA Modules:
  0.0 247.8 jit_solution(17410104126802785605)
XLA Ops:
  0.6 3.7 %multiply_add_fusion = f32[512,2,512]{2,1,0:T(2,128)S(1)} fusion(f32[512,2,512]{2,1,0:T(2,128)} %param.3, f32[512,2,512]{2,1,0:T(2,128)} %param.4), kind=kLoop, calls=%fused_computation.8 | loop fusion | flops 1048576 | bytes 6291456 | tf_op jit(solution)/shard_map/add | solution.py:20
  4.3 63.1 %all_to_all.59 = f32[512,2,512]{2,1,0:T(2,128)S(1)} all-to-all(f32[512,2,512]{2,1,0:T(2,128)S(1)} %multiply_add_fusion), channel_id=1, replica_groups=mesh['shard'=64,'model'=4] {'shard'}, dimensions={0} | all-to-all | bytes 4194304 | tf_op jit(solution)/shard_map/all_to_all | solution.py:21
  68.0 1.2 copy.22
  69.2 29.1 %all_to_all.60 = f32[8,128,512]{2,1,0:T(8,128)S(1)} all-to-all(f32[8,128,512]{2,1,0:T(8,128)S(1)} %copy.22), channel_id=1, replica_groups=mesh['shard'=64,'model'=4] {'model'}, dimensions={0} | all-to-all | bytes 4194304 | tf_op jit(solution)/shard_map/all_to_all | solution.py:22
  98.9 2.3 fusion
  101.5 2.1 convolution_add_fusion.4
  103.6 2.0 fusion.10
  105.9 2.1 convolution_add_fusion.3
  108.1 2.0 fusion.11
  110.4 2.3 convolution_add_fusion.2
  112.7 2.0 fusion.12
  115.0 2.1 convolution_add_fusion.1
  117.1 2.0 fusion.13
  119.4 2.1 convolution_add_fusion
  121.5 2.3 copy.24
  123.9 27.5 %all_to_all.61 = f32[2,128,2048]{1,0,2:T(2,128)S(1)} all-to-all(f32[2,128,2048]{1,0,2:T(2,128)} %copy.24), channel_id=1, replica_groups=mesh['shard'=64,'model'=4] {'model'}, dimensions={2} | all-to-all | bytes 4194304 | tf_op jit(solution)/shard_map/all_to_all | solution.py:32
  151.5 1.8 copy.26
  153.3 1.1 constant_dynamic-update-slice_fusion.63
  159.0 0.9 constant_dynamic-update-slice_fusion.57
  160.0 0.9 constant_dynamic-update-slice_fusion.56
  162.8 0.9 constant_dynamic-update-slice_fusion.53
  163.7 0.9 constant_dynamic-update-slice_fusion.52
  166.5 0.9 constant_dynamic-update-slice_fusion.49
  167.4 0.9 constant_dynamic-update-slice_fusion.48
  170.2 0.9 constant_dynamic-update-slice_fusion.45
  171.1 0.9 constant_dynamic-update-slice_fusion.44
  173.9 0.9 constant_dynamic-update-slice_fusion.41
  174.8 0.9 constant_dynamic-update-slice_fusion.40
  177.6 0.9 constant_dynamic-update-slice_fusion.37
  178.5 0.9 constant_dynamic-update-slice_fusion.36
  184.1 60.4 %all_to_all.62 = f32[64,8,2,512]{3,2,1,0:T(2,128)S(1)} all-to-all(f32[64,8,2,512]{3,2,1,0:T(2,128)S(1)} %constant_dynamic-update-slice_fusion), channel_id=1, replica_groups=mesh['shard'=64,'model'=4] {'shard'}, dimensions={0} | all-to-all | bytes 4194304 | tf_op jit(solution)/shard_map/all_to_all | solution.py:15
  244.5 3.3 %bitcast_subtract_fusion = f32[512,2,512]{2,1,0:T(2,128)} fusion(f32[64,8,2,512]{3,2,1,0:T(2,128)S(1)} %all_to_all.62, f32[512,2,512]{2,1,0:T(2,128)S(1)} %copy-done.2), kind=kLoop, calls=%fused_computation.5 | loop fusion | flops 1048576 | bytes 6291456 | tf_op jit(solution)/shard_map/sub | solution.py:34
  (68 shorter events, 21.1 us)
Async XLA Ops:
  4.3 63.5 %copy-start = (f32[512,2,512]{2,1,0:T(2,128)}, f32[512,2,512]{2,1,0:T(2,128)S(1)}, u32[]{:S(2)}) copy-start(f32[512,2,512]{2,1,0:T(2,128)S(1)} %multiply_add_fusion) | copy-start | bytes 6291460
  153.3 29.9 %copy-start.1 = (f32[4,2,128,512]{3,2,1,0:T(8,128)S(1)}, f32[4,2,128,512]{3,2,1,0:T(8,128)}, u32[]{:S(2)}) copy-start(f32[4,2,128,512]{3,2,1,0:T(8,128)} %copy.26) | copy-start | bytes 6291460
  184.1 60.5 %copy-start.2 = (f32[512,2,512]{2,1,0:T(2,128)S(1)}, f32[512,2,512]{2,1,0:T(2,128)}, u32[]{:S(2)}) copy-start(f32[512,2,512]{2,1,0:T(2,128)} %param.5) | copy-start | bytes 6291460
